TPU v7x, 32 devices: a whole 2x2x4 slice. The times are simulated.
32 devices in a mesh: win: 4 (over x, core), obs: 8 (over z, y).
Axes of the slice: x: 2, y: 2, z: 4, core: 2. Of those that a mesh axis runs over, the one named last changes fastest.
Arguments:
- predictors: float32 [4, 8, 262144], P('win', None, 'obs'), may hold values from -8 to 8
- departures: float32 [4, 262144], P('win', 'obs'), may hold values from -30 to 30
- channel: int32 [4, 262144], P('win', 'obs'), may hold values from 0 to 299
- decay_rate: float32 [4, 300], P('win'), may hold values from 0.5 to 1
- ridge_counts: int32 [4, 300], P('win'), may hold values from 219 to 874
Outputs:
- coefficients: float32 [4, 8, 300], P('win')
- corrected: float32 [4, 262144], P('win', 'obs')
All inputs are finite; a program needn't handle non-finite values.
Results may differ from a plain program's by a relative error of at most 0.00013.
Values sent between devices are 32-bit elements; how exact they have to be, the bound alone decides.
A program may use at most 64 MiB of HBM per device.

v0:
```python
import jax
import jax.numpy as jnp
from jax import lax
from jax.sharding import PartitionSpec as P

ROUNDS = 3


huber_edge = 1.5


def block_indicator(labels_here, channels):
    channel_ids = jnp.arange(channels, dtype=jnp.int32)
    return (labels_here[:, None] == channel_ids[None, :]).astype(jnp.float32)


def block_fit(columns, coeffs, indicator):
    spread = lax.dot_general(
        coeffs,
        indicator,
        (((1,), (1,)), ((), ())),
        precision=lax.Precision.HIGHEST,
        preferred_element_type=jnp.float32,
    )
    return jnp.sum(columns * spread, axis=0)


def build_features(predictors, departure, weights):
    weighted = predictors * weights[None, :]
    gram_rows = (weighted[:, None, :] * predictors[None, :, :]).reshape(-1, predictors.shape[1])
    moment_rows = weighted * departure[None, :]
    return jnp.concatenate([gram_rows, moment_rows], axis=0)


def round_statistics(rows_here, departure, labels_all, coeffs, channels):
    total_rows = rows_here.shape[1]
    dimension = rows_here.shape[0]
    block_size = min(2048, total_rows)

    def add_block(position, running):
        begin = position * block_size
        columns = lax.dynamic_slice_in_dim(rows_here, begin, block_size, 1)
        depart_here = lax.dynamic_slice_in_dim(departure, begin, block_size, 0)
        labels_here = lax.dynamic_slice_in_dim(labels_all, begin, block_size, 0)
        indicator = block_indicator(labels_here, channels)
        residual = depart_here - block_fit(columns, coeffs, indicator)
        weights = huber_edge / jnp.maximum(jnp.abs(residual), huber_edge)
        features = build_features(columns, depart_here, weights)
        return running + jnp.dot(
            features, indicator, precision=lax.Precision.HIGHEST, preferred_element_type=jnp.float32
        )

    initial = jnp.zeros((dimension * dimension + dimension, channels), jnp.float32)
    return lax.fori_loop(0, total_rows // block_size, add_block, initial)


def final_correction(rows_here, departure, labels_all, coeffs, channels):
    total_rows = rows_here.shape[1]
    block_size = min(2048, total_rows)

    def fill_block(position, output):
        begin = position * block_size
        columns = lax.dynamic_slice_in_dim(rows_here, begin, block_size, 1)
        depart_here = lax.dynamic_slice_in_dim(departure, begin, block_size, 0)
        labels_here = lax.dynamic_slice_in_dim(labels_all, begin, block_size, 0)
        indicator = block_indicator(labels_here, channels)
        values = depart_here - block_fit(columns, coeffs, indicator)
        return lax.dynamic_update_slice_in_dim(output, values, begin, 0)

    return lax.fori_loop(0, total_rows // block_size, fill_block, jnp.zeros_like(departure))


def solve_small(matrix, right_side):
    dimension = right_side.shape[0]
    factor = {}
    for column in range(dimension):
        pivot_square = matrix[column, column] - sum(
            (factor[column, middle] * factor[column, middle] for middle in range(column))
        )
        pivot_root = jnp.sqrt(pivot_square)
        factor[column, column] = pivot_root
        for row_index in range(column + 1, dimension):
            partial_sum = matrix[row_index, column] - sum(
                (factor[row_index, middle] * factor[column, middle] for middle in range(column))
            )
            factor[row_index, column] = partial_sum / pivot_root
    forward = []
    for row_index in range(dimension):
        entry_value = right_side[row_index] - sum(
            (factor[row_index, middle] * forward[middle] for middle in range(row_index))
        )
        forward.append(entry_value / factor[row_index, row_index])
    solution = [None] * dimension
    for row_index in reversed(range(dimension)):
        entry_value = forward[row_index] - sum(
            (
                factor[middle, row_index] * solution[middle]
                for middle in range(row_index + 1, dimension)
            )
        )
        solution[row_index] = entry_value / factor[row_index, row_index]
    return jnp.stack(solution, axis=0)


def solve_channels(summed, ridges, dimension):
    matrix = summed[: dimension * dimension].reshape(dimension, dimension, -1)
    matrix = matrix + ridges[None, None, :] * jnp.eye(dimension, dtype=jnp.float32)[:, :, None]
    return solve_small(matrix, summed[dimension * dimension :])


def chain_windows(summed, decays):
    all_decays, all_summed = (
        lax.all_gather(decays[None], "win", axis=0, tiled=True),
        lax.all_gather(summed[None], "win", axis=0, tiled=True),
    )
    position = lax.axis_index("win")
    carried = jnp.zeros_like(summed)
    kept = jnp.zeros_like(summed)
    for window in range(lax.axis_size("win")):
        carried = all_decays[window][None, :] * carried + all_summed[window]
        kept = jnp.where(position == window, carried, kept)
    return kept


def body(predictors, departures, channel, decay_rate, ridge_counts):
    channels = decay_rate.shape[1]
    dimension = predictors.shape[1]
    rows_here = predictors[0]
    departure = departures[0]
    labels_all = channel[0]
    decays = decay_rate[0]
    ridges = ridge_counts[0].astype(jnp.float32)
    coeffs = jnp.zeros((dimension, channels), jnp.float32)
    for round_index in range(ROUNDS):
        summed = round_statistics(rows_here, departure, labels_all, coeffs, channels)
        summed = lax.psum(summed, "obs")
        chained = chain_windows(summed, decays)
        coeffs = solve_channels(chained, ridges, dimension)
    corrected = final_correction(rows_here, departure, labels_all, coeffs, channels)
    return (coeffs[None], corrected[None])


def solution(mesh):
    placed = (
        P("win", None, "obs"),
        P("win", "obs"),
        P("win", "obs"),
        P("win", None),
        P("win", None),
    )
    return jax.shard_map(
        body,
        mesh=mesh,
        in_specs=placed,
        out_specs=(P("win", None, None), P("win", "obs")),
        check_vma=False,
    )
```

profile of v0, /device:TPU:0, one launch (start us, length us, event | category | flops | bytes accessed | tf_op | source)
XLA Modules:
  0.0 605.2 jit_solution(720842672770661011)
XLA Ops:
  7.2 98.0 %while.56 = (s32[]{:T(128)}, f32[72,300]{1,0:T(8,128)S(1)}, f32[8,32768]{1,0:T(8,128)}, f32[32768]{0:T(1024)}, s32[32768]{0:T(1024)}, /*index=5*/s32[]{:T(128)}, s32[]{:T(128)}, s32[]{:T(128)}, s32[]{:T(128)}) while((s32[]{:T(128)}, f32[72,300]{1,0:T(8,128)S(1)}, f32[8,32768]{1,0:T(8,128)}, f32[32768]{0:T(1024)}, s32[32768]{0:T(1024)}, ...), condition=%wide.region_2.0_spmd.clone, body=%wide.region_0.0_spmd.clone.sunk | while | flops 591446208 | bytes 1901477 | solution.py:54
  106.0 6.1 %all-gather = f32[4,1,300]{2,1,0:T(1,128)S(1)} all-gather(f32[1,1,300]{2,1,0:T(1,128)S(1)} %bitcast.1220), channel_id=1, replica_groups=mesh['win'=4,'obs'=8] {'win'}, dimensions={0}, use_global_device_ids=true | all-gather | bytes 6000 | tf_op jit(solution)/shard_map/all_gather | solution.py:113
  112.2 66.1 %all-reduce.4.cloned.1.call-done = f32[1,72,300]{2,1,0:T(8,128)} async-done(((f32[1,72,300]{2,1,0:T(8,128)}), f32[1,72,300]{2,1,0:T(8,128)}) %all-reduce.4.cloned.1.call-update) | async-done | bytes 86416 | tf_op jit(solution)/shard_map/psum | solution.py:136
  178.4 6.9 %all_gather.15 = f32[4,72,300]{2,1,0:T(8,128)S(1)} all-gather(f32[1,72,300]{2,1,0:T(8,128)} %all-reduce.4.cloned.1.call-done), channel_id=1, replica_groups=mesh['win'=4,'obs'=8] {'win'}, dimensions={0}, use_global_device_ids=true | all-gather | bytes 432000 | tf_op jit(solution)/shard_map/all_gather | solution.py:114
  185.9 98.0 %while.57 = (s32[]{:T(128)}, f32[72,300]{1,0:T(8,128)S(1)}, f32[8,32768]{1,0:T(8,128)}, f32[32768]{0:T(1024)}, s32[32768]{0:T(1024)}, /*index=5*/f32[8,300]{1,0:...) while((s32[]{:T(128)}, f32[72,300]{1,0:T(8,128)S(1)}, f32[8,32768]{1,0:T(8,128)}, ...), condition=%wide.region_6.7_spmd.clone, body=%wide.region_4.6_spmd.clone.sunk | while | flops 591446208 | bytes 1911085 | solution.py:54
  284.7 69.2 %all-reduce.6.cloned.1.call-done = f32[1,72,300]{2,1,0:T(8,128)} async-done(((f32[1,72,300]{2,1,0:T(8,128)}), f32[1,72,300]{2,1,0:T(8,128)}) %all-reduce.6.cloned.1.call-update) | async-done | bytes 86416 | tf_op jit(solution)/shard_map/psum | solution.py:136
  353.9 6.9 %all_gather.16 = f32[4,72,300]{2,1,0:T(8,128)S(1)} all-gather(f32[1,72,300]{2,1,0:T(8,128)} %all-reduce.6.cloned.1.call-done), channel_id=1, replica_groups=mesh['win'=4,'obs'=8] {'win'}, dimensions={0}, use_global_device_ids=true | all-gather | bytes 432000 | tf_op jit(solution)/shard_map/all_gather | solution.py:114
  361.4 98.0 %while.58 = (s32[]{:T(128)}, f32[72,300]{1,0:T(8,128)S(1)}, f32[8,32768]{1,0:T(8,128)}, f32[32768]{0:T(1024)}, s32[32768]{0:T(1024)}, /*index=5*/f32[8,300]{1,0:...) while((s32[]{:T(128)}, f32[72,300]{1,0:T(8,128)S(1)}, f32[8,32768]{1,0:T(8,128)}, ...), condition=%wide.region_10.11_spmd.clone, body=%wide.region_8.10_spmd.clone.sunk | while | flops 591446208 | bytes 1911085 | solution.py:54
  460.2 69.2 %all-reduce.8.cloned.1.call-done = f32[1,72,300]{2,1,0:T(8,128)} async-done(((f32[1,72,300]{2,1,0:T(8,128)}), f32[1,72,300]{2,1,0:T(8,128)}) %all-reduce.8.cloned.1.call-update) | async-done | bytes 86416 | tf_op jit(solution)/shard_map/psum | solution.py:136
  529.4 6.9 %all_gather.17 = f32[4,72,300]{2,1,0:T(8,128)S(1)} all-gather(f32[1,72,300]{2,1,0:T(8,128)} %all-reduce.8.cloned.1.call-done), channel_id=1, replica_groups=mesh['win'=4,'obs'=8] {'win'}, dimensions={0}, use_global_device_ids=true | all-gather | bytes 432000 | tf_op jit(solution)/shard_map/all_gather | solution.py:114
  536.9 61.0 %while.55 = (s32[]{:T(128)}, f32[32768]{0:T(1024)S(1)}, f32[32768]{0:T(1024)}, f32[8,32768]{1,0:T(8,128)}, s32[32768]{0:T(1024)}, /*index=5*/f32[8,300]{1,0:T(8,...) while((s32[]{:T(128)}, f32[32768]{0:T(1024)S(1)}, f32[32768]{0:T(1024)}, f32[8,32768]{1,0:T(8,128)}, ...), condition=%wide.region_14.15_spmd, body=%wide.region_12.14_spmd.sunk | while | flops 59629572 | bytes 132639 | solution.py:70
  537.7 2.4 fusion.248
  541.5 2.4 fusion.248
  545.3 2.4 fusion.248
  549.1 2.4 fusion.248
  552.9 2.4 fusion.248
  556.7 2.4 fusion.248
  564.4 2.4 fusion.248
  568.2 2.4 fusion.248
  572.0 2.4 fusion.248
  575.8 2.4 fusion.248
  583.4 2.4 fusion.248
  591.0 2.4 fusion.248
  594.9 2.4 fusion.248
  (416 shorter events, 326.1 us)
Async XLA Ops:
  7.2 171.2 %all-reduce.4.cloned.1.call-start = ((), (), s32[]{:S(2)}) async-start(), calls=%async_computation | async-start | bytes 221184 | tf_op jit(solution)/shard_map/psum | solution.py:136
  7.2 98.8 %copy-start.6 = (f32[1,300]{1,0:T(1,128)S(1)}, f32[1,300]{1,0:T(1,128)}, u32[]{:S(2)}) copy-start(f32[1,300]{1,0:T(1,128)} %param.16) | copy-start | bytes 3604
  7.2 105.0 %copy-start.5 = (s32[1,300]{1,0:T(1,128)S(1)}, s32[1,300]{1,0:T(1,128)}, u32[]{:S(2)}) copy-start(s32[1,300]{1,0:T(1,128)} %param.17) | copy-start | bytes 3604
  105.3 0.6 copy-start.3
  105.9 247.9 %all-reduce.6.cloned.1.call-start = ((), (), s32[]{:S(2)}) async-start(), calls=%async_computation.1 | async-start | bytes 221184 | tf_op jit(solution)/shard_map/psum | solution.py:136
  284.0 0.6 copy-start.1
  284.6 244.7 %all-reduce.8.cloned.1.call-start = ((), (), s32[]{:S(2)}) async-start(), calls=%async_computation.2 | async-start | bytes 221184 | tf_op jit(solution)/shard_map/psum | solution.py:136
  459.5 0.6 copy-start.2
  598.0 0.7 copy-start
  598.0 0.7 copy-start.4
Sparse Core Ops, SparseCore 0:
  106.1 72.2 all-reduce.3
  284.8 69.0 all-reduce.5
  460.3 69.0 all-reduce.7
where the time goes:
time: 616 us; the launch traced here: 605 us
  waiting for transfers between devices  205 us (33%)
  matrix products  178 us (29%)
  other arithmetic  90.6 us (15%)
  local copies, waits for them, and re-layouts  88.1 us (14%)
  blocking collectives  26.8 us (4%)
  between operations  13.9 us (2%)
    psum x3, waiting for transfers between devices, body(): summed = lax.psum(summed, 'obs')  204 us
    dot_general x64, matrix products, block_fit(): lax.dot_general(coeffs, indicator, (((1,), (1,)), ((), ())), precision=la...  113 us
    dot_general x48, matrix products, add_block(): jnp.dot(features, indicator, precision=lax.Precision.HIGHEST, preferred_e...  65.1 us
    mul x48, other arithmetic, build_features(): moment_rows = weighted * departure[None, :]  41.1 us
    dynamic_slice x48, local copies, waits for them, and re-layouts, add_block(): columns = lax.dynamic_slice_in_dim(rows_here, begin, block_size, 1)  40.7 us
    div x48, other arithmetic, add_block(): weights = huber_edge / jnp.maximum(jnp.abs(residual), huber_edge)  34.2 us
    dynamic_slice x48, local copies, waits for them, and re-layouts, add_block(): labels_here = lax.dynamic_slice_in_dim(labels_all, begin, block_size, 0)  33.5 us
    all_gather x3, blocking collectives, chain_windows(): lax.all_gather(summed[None], 'win', axis=0, tiled=True)  20.7 us
  transfers between devices with their start and end apart: 3, of which 3 were waited for; matrix products, arithmetic and copies ran while one was open for 0% of the time, Pallas kernels for 0%

commit v1 on v0

v1 whole, which is shorter than its diff:
```python
import functools

import jax
import jax.numpy as jnp
from jax import lax
from jax.experimental import pallas as pl
from jax.experimental.pallas import tpu as pltpu
from jax.sharding import PartitionSpec as P

ROUNDS = 3
LANES = 128
GROUPS = 16

huber_edge = 1.5

MESH = pl.DeviceIdType.MESH


def ceil_to(value, unit):
    return (value + unit - 1) // unit * unit


def gather_lanes(table, index):
    return jnp.take_along_axis(table, index, axis=1, mode="promise_in_bounds")


def fit_group(columns, labels, tables):
    low = jnp.bitwise_and(labels, LANES - 1)
    high = jnp.right_shift(labels, 7)
    picked = gather_lanes(tables[0], low)
    for slab in range(1, len(tables)):
        picked = jnp.where(high == slab, gather_lanes(tables[slab], low), picked)
    return jnp.sum(columns * picked, axis=0, keepdims=True)


def entry_place(a, b, dim):
    shift = (a - b) % dim
    if shift <= dim // 2:
        return shift * dim + a
    return (dim - shift) * dim + b


def kernel(
    sizes,
    rows_ref,
    depart_ref,
    label_ref,
    decay_ref,
    ridge_ref,
    coef_ref,
    corrected_ref,
    acc,
    stats,
    beta,
    ridge_row,
    decays,
    parts,
    totals,
    chained,
    decay_send,
    decay_recv,
    part_send,
    part_recv,
    total_send,
    total_recv,
    chain_send,
    chain_recv,
):
    dim, channels, n_win, n_obs, slabs = sizes
    width = slabs * LANES
    hot_rows = ceil_to(channels, 16)
    owners = stats.shape[0] // dim
    steps = depart_ref.shape[0] // GROUPS
    chunk = GROUPS * LANES
    w = lax.axis_index("win")
    o = lax.axis_index("obs")

    barrier = pltpu.get_barrier_semaphore()
    for step in range(1, n_obs):
        pl.semaphore_signal(
            barrier, inc=1, device_id={"obs": lax.rem(o + step, n_obs)}, device_id_type=MESH
        )
    for step in range(1, n_win):
        pl.semaphore_signal(
            barrier, inc=1, device_id={"win": lax.rem(w + step, n_win)}, device_id_type=MESH
        )
    pl.semaphore_wait(barrier, n_obs + n_win - 2)

    def decay_copy(step, slot, target):
        return pltpu.make_async_remote_copy(
            src_ref=decays.at[slot],
            dst_ref=decays.at[slot],
            send_sem=decay_send.at[step],
            recv_sem=decay_recv.at[step],
            device_id={"win": target},
            device_id_type=MESH,
        )

    decays[w] = jnp.zeros((dim, width), jnp.float32)
    decays[w, :, 0:channels] = jnp.broadcast_to(decay_ref[...], (dim, channels))
    for step in range(1, n_win):
        decay_copy(step, w, lax.rem(w + step, n_win)).start()

    ridge_row[...] = jnp.ones_like(ridge_row)
    ridge_row[:, 0:channels] = ridge_ref[...].astype(jnp.float32)
    beta[...] = jnp.zeros_like(beta)

    def tables_now():
        return [beta[:, slab * LANES : (slab + 1) * LANES] for slab in range(slabs)]

    def wide_row(ref, row):
        return jnp.broadcast_to(ref[pl.ds(row, 1), :], (dim, LANES))

    def accumulate(step, tables):
        fits, departs, labels = [], [], []
        columns_all = []
        for group in range(GROUPS):
            row = step * GROUPS + group
            begin = pl.multiple_of(row * LANES, LANES)
            columns = rows_ref[:, pl.ds(begin, LANES)]
            label = wide_row(label_ref, row)
            depart = wide_row(depart_ref, row)
            residual = depart - fit_group(columns, label, tables)
            weight = huber_edge / jnp.maximum(jnp.abs(residual), huber_edge)
            columns_all.append(columns)
            fits.append(columns * weight)
            departs.append(depart)
            labels.append(label)
        columns = jnp.concatenate(columns_all, axis=1)
        weighted = jnp.concatenate(fits, axis=1)
        depart = jnp.concatenate(departs, axis=1)
        label = jnp.concatenate(labels, axis=1)
        features = [weighted * columns]
        for shift in range(1, dim // 2 + 1):
            features.append(weighted * pltpu.roll(columns, shift, axis=0))
        features.append(weighted * depart)
        features = jnp.concatenate(features, axis=0)
        high = features.astype(jnp.bfloat16)
        low = (features - high.astype(jnp.float32)).astype(jnp.bfloat16)
        pair = jnp.concatenate([high, low], axis=0)
        hots = []
        one, nought = jnp.bfloat16(1), jnp.bfloat16(0)
        for base in range(0, hot_rows, 256):
            here = min(256, hot_rows - base)
            shifted = (label - base).astype(jnp.float32).astype(jnp.bfloat16)
            ids = lax.broadcasted_iota(jnp.int32, (here, LANES), 0)
            ids = ids.astype(jnp.float32).astype(jnp.bfloat16)
            shifted16 = jnp.concatenate([shifted, shifted], axis=0)
            for part in range(0, here, 2 * dim):
                id_tile = jnp.concatenate([ids[part : part + 2 * dim]] * GROUPS, axis=1)
                hots.append(jnp.where(id_tile == shifted16, one, nought))
        hot = jnp.concatenate(hots, axis=0)
        acc[:, 0:hot_rows] += lax.dot_general(
            pair, hot, (((1,), (1,)), ((), ())), preferred_element_type=jnp.float32
        )

    def part_copy(r, group, slot):
        return pltpu.make_async_remote_copy(
            src_ref=stats.at[pl.ds(group * dim, dim)],
            dst_ref=parts.at[r, slot],
            send_sem=part_send.at[r, group],
            recv_sem=part_recv.at[r, slot],
            device_id={"obs": group},
            device_id_type=MESH,
        )

    def total_copy(r, step, slot, target):
        return pltpu.make_async_remote_copy(
            src_ref=totals.at[r, slot],
            dst_ref=totals.at[r, slot],
            send_sem=total_send.at[r, step],
            recv_sem=total_recv.at[r, step],
            device_id={"win": target},
            device_id_type=MESH,
        )

    def chain_copy(r, step, slot, target):
        return pltpu.make_async_remote_copy(
            src_ref=chained.at[r, slot],
            dst_ref=chained.at[r, slot],
            send_sem=chain_send.at[r, step],
            recv_sem=chain_recv.at[r, slot],
            device_id={"obs": target},
            device_id_type=MESH,
        )

    def combine(r):
        half = stats.shape[0]
        stats[...] = acc[0:half] + acc[half:]
        for group in range(owners):

            @pl.when(o != group)
            def _():
                part_copy(r, group, o).start()

        @pl.when(o < owners)
        def _():
            parts[r, o] = stats[pl.ds(pl.multiple_of(o * dim, dim), dim), :]
            for step in range(1, n_obs):
                part_copy(r, 0, lax.rem(o + step, n_obs)).wait_recv()
            total = parts[r, 0]
            for source in range(1, n_obs):
                total = total + parts[r, source]
            totals[r, w] = total
            for step in range(1, n_win):
                total_copy(r, step, w, lax.rem(w + step, n_win)).start()
            for step in range(1, n_win):
                total_copy(r, step, lax.rem(w + n_win - step, n_win), w).wait_recv()
            carried = totals[r, 0]
            for window in range(1, n_win):
                further = decays[window] * carried + totals[r, window]
                carried = jnp.where(window <= w, further, carried)
            chained[r, o] = carried
            for step in range(1, n_obs):
                chain_copy(r, step, o, lax.rem(o + step, n_obs)).start()

        for group in range(owners):

            @pl.when(o != group)
            def _():
                chain_copy(r, 1, group, o).wait_recv()

        for group in range(owners):

            @pl.when(o != group)
            def _():
                part_copy(r, group, o).wait_send()

        @pl.when(o < owners)
        def _():
            for step in range(1, n_win):
                total_copy(r, step, w, w).wait_send()
            for step in range(1, n_obs):
                chain_copy(r, step, o, o).wait_send()

    def solve(r):
        def entry(place):
            return chained[r, place // dim, pl.ds(place % dim, 1), :]

        unit = {}
        scaled = {}
        inverse = []
        for column in range(dim):
            pivot = entry(entry_place(column, column, dim)) + ridge_row[...]
            for middle in range(column):
                pivot = pivot - unit[column, middle] * scaled[column, middle]
            inverse.append(1.0 / pivot)
            for row in range(column + 1, dim):
                value = entry(entry_place(row, column, dim))
                for middle in range(column):
                    value = value - unit[column, middle] * scaled[row, middle]
                scaled[row, column] = value
                unit[row, column] = value * inverse[column]
        forward = []
        moment = (dim // 2 + 1) * dim
        for row in range(dim):
            value = entry(moment + row)
            for middle in range(row):
                value = value - unit[row, middle] * forward[middle]
            forward.append(value)
        answer = [None] * dim
        for row in reversed(range(dim)):
            value = forward[row] * inverse[row]
            for middle in range(row + 1, dim):
                value = value - unit[middle, row] * answer[middle]
            answer[row] = value
            beta[row : row + 1, :] = value

    for step in range(1, n_win):
        decay_copy(step, lax.rem(w + n_win - step, n_win), w).wait_recv()
    for step in range(1, n_win):
        decay_copy(step, w, w).wait_send()

    def one_round(r, carry):
        acc[...] = jnp.zeros_like(acc)
        tables = tables_now()

        def one_step(step, inner):
            accumulate(step, tables)
            return inner

        lax.fori_loop(0, steps, one_step, 0)
        combine(r)
        solve(r)
        return carry

    lax.fori_loop(0, ROUNDS, one_round, 0)

    coef_ref[...] = beta[:, 0:channels]
    tables = tables_now()

    def correct(step, carry):
        for group in range(GROUPS):
            row = step * GROUPS + group
            begin = pl.multiple_of(row * LANES, LANES)
            columns = rows_ref[:, pl.ds(begin, LANES)]
            fitted = fit_group(columns, wide_row(label_ref, row), tables)
            corrected_ref[pl.ds(row, 1), :] = depart_ref[pl.ds(row, 1), :] - fitted
        return carry

    lax.fori_loop(0, steps, correct, 0)


def body(n_win, n_obs, predictors, departures, channel, decay_rate, ridge_counts):
    channels = decay_rate.shape[1]
    dim = predictors.shape[1]
    total_rows = predictors.shape[2]
    slabs = ceil_to(channels, LANES) // LANES
    width = slabs * LANES
    owners = dim // 2 + 2
    packed = owners * dim
    assert n_obs >= owners and total_rows % (GROUPS * LANES) == 0
    vmem = pl.BlockSpec(memory_space=pltpu.VMEM)
    dma = pltpu.SemaphoreType.DMA
    coeffs, corrected = pl.pallas_call(
        functools.partial(kernel, (dim, channels, n_win, n_obs, slabs)),
        out_shape=(
            jax.ShapeDtypeStruct((dim, channels), jnp.float32),
            jax.ShapeDtypeStruct((total_rows // LANES, LANES), jnp.float32),
        ),
        in_specs=[vmem] * 5,
        out_specs=(vmem, vmem),
        scratch_shapes=[
            pltpu.VMEM((2 * packed, width), jnp.float32),
            pltpu.VMEM((packed, width), jnp.float32),
            pltpu.VMEM((dim, width), jnp.float32),
            pltpu.VMEM((1, width), jnp.float32),
            pltpu.VMEM((n_win, dim, width), jnp.float32),
            pltpu.VMEM((ROUNDS, n_obs, dim, width), jnp.float32),
            pltpu.VMEM((ROUNDS, n_win, dim, width), jnp.float32),
            pltpu.VMEM((ROUNDS, owners, dim, width), jnp.float32),
            dma((n_win,)),
            dma((n_win,)),
            dma((ROUNDS, owners)),
            dma((ROUNDS, n_obs)),
            dma((ROUNDS, n_win)),
            dma((ROUNDS, n_win)),
            dma((ROUNDS, n_obs)),
            dma((ROUNDS, owners)),
        ],
        compiler_params=pltpu.CompilerParams(
            collective_id=0, has_side_effects=True, vmem_limit_bytes=48 * 1024 * 1024
        ),
    )(
        predictors.reshape(dim, total_rows),
        departures.reshape(total_rows // LANES, LANES),
        channel.reshape(total_rows // LANES, LANES),
        decay_rate,
        ridge_counts,
    )
    return (coeffs[None], corrected.reshape(1, total_rows))


def solution(mesh):
    placed = (
        P("win", None, "obs"),
        P("win", "obs"),
        P("win", "obs"),
        P("win", None),
        P("win", None),
    )
    return jax.shard_map(
        functools.partial(body, mesh.shape["win"], mesh.shape["obs"]),
        mesh=mesh,
        in_specs=placed,
        out_specs=(P("win", None, None), P("win", "obs")),
        check_vma=False,
    )
```

time: 616 us -> 81.7 us (0.13); the launches traced: 605 us -> 81.5 us
  waiting for transfers between devices: 205 us -> 0 us
  matrix products: 178 us -> 0 us
  other arithmetic: 90.6 us -> 0 us
  local copies, waits for them, and re-layouts: 88.1 us -> 4.97 us
  Pallas kernels: 0 us -> 75.9 us
  blocking collectives: 26.8 us -> 0 us
  between operations: 13.9 us -> 0.66 us
    psum x3 -> x0, waiting for transfers between devices: 204 us -> none  [body(): summed = lax.psum(summed, 'obs')]
    dot_general x112 -> x0, matrix products: 178 us -> none  [the longest x64 113 us: block_fit(): lax.dot_general(coeffs, indicator, (((1,), (1,)), ((), ())), precision=la...]
    dynamic_slice x112 -> x0, local copies, waits for them, and re-layouts: 85.4 us -> none  [the longest x48 40.7 us: add_block(): columns = lax.dynamic_slice_in_dim(rows_here, begin, block_size, 1)]
    pallas_call x0 -> x1, Pallas kernels: none -> 75.9 us  [body(): pl.pallas_call(functools.partial(kernel, (dim, channels, n_win, n_obs, sl...]
    mul x96 -> x0, other arithmetic: 43.2 us -> none  [the longest x48 41.1 us: build_features(): moment_rows = weighted * departure[None, :]]
    div x57 -> x0, other arithmetic: 35.7 us -> none  [the longest x48 34.2 us: add_block(): weights = huber_edge / jnp.maximum(jnp.abs(residual), huber_edge)]
    all_gather x4 -> x0, blocking collectives: 26.8 us -> none  [the longest x3 20.7 us: chain_windows(): lax.all_gather(summed[None], 'win', axis=0, tiled=True)]
    dynamic_update_slice x16 -> x0, other arithmetic: 11.3 us -> none  [fill_block(): return lax.dynamic_update_slice_in_dim(output, values, begin, 0)]
  transfers between devices with their start and end apart: 3 -> 0, of which waited for: 3 -> 0; matrix products, arithmetic and copies ran while one was open for 0% -> 0% of each run, Pallas kernels for 0% -> 0%
where the time goes in v1:
time: 81.7 us; the launch traced here: 81.5 us
  Pallas kernels  75.9 us (93%)
  local copies, waits for them, and re-layouts  4.97 us (6%)
    pallas_call x1, Pallas kernels, body(): pl.pallas_call(functools.partial(kernel, (dim, channels, n_win, n_obs, sl...  75.9 us
    unnamed x12, local copies, waits for them, and re-layouts  4.97 us

profile of v1, /device:TPU:0, one launch (start us, length us, event | category | flops | bytes accessed | tf_op | source)
XLA Modules:
  0.0 81.5 jit_solution(5357600784315569953)
XLA Ops:
  0.6 0.0 copy-start.3
  0.6 0.0 copy-start.4
  0.7 0.7 copy-done.3
  1.3 0.0 copy-done.4
  1.3 0.0 copy-start
  1.3 1.2 %copy-done = f32[1,8,32768]{2,1,0:T(8,128)S(1)} copy-done((f32[1,8,32768]{2,1,0:T(8,128)S(1)}, f32[1,8,32768]{2,1,0:T(8,128)}, u32[]{:S(2)}) %copy-start) | copy-done | bytes 1048600
  2.6 0.0 copy-start.1
  2.6 0.9 %copy-done.1 = f32[1,32768]{1,0:T(1,128)S(1)} copy-done((f32[1,32768]{1,0:T(1,128)S(1)}, f32[1,32768]{1,0:T(1,128)}, u32[]{:S(2)}) %copy-start.1) | copy-done | bytes 131096
  3.5 0.0 copy-start.2
  3.5 0.9 %copy-done.2 = s32[1,32768]{1,0:T(1,128)S(1)} copy-done((s32[1,32768]{1,0:T(1,128)S(1)}, s32[1,32768]{1,0:T(1,128)}, u32[]{:S(2)}) %copy-start.2) | copy-done | bytes 131096
  4.4 75.9 %shard_map.68 = (f32[8,300]{1,0:T(8,128)S(1)}, f32[256,128]{1,0:T(8,128)S(1)}) custom-call(f32[8,32768]{1,0:T(8,128)S(1)} %bitcast.5, f32[256,128]{1,0:T(8,128)S(1)} %bitcast.6, s32[256,128]{1,0:T(8,128)S(1)} %bitcast.7, f32[1,300]{1,0:T(1,128)S(1)} %copy-done.3, s32[1,300]{1,0:T(1,128)S(1)} %copy-done.4), custom_call_target="tpu_custom_call" | custom-call | tf_op jit(solution)/shard_map/pallas_call | solution.py:315
  80.3 0.6 copy.9
  80.9 0.7 copy.10
Async XLA Ops:
  0.6 0.7 copy-start.3
  0.6 0.7 copy-start.4
  1.3 1.2 %copy-start = (f32[1,8,32768]{2,1,0:T(8,128)S(1)}, f32[1,8,32768]{2,1,0:T(8,128)}, u32[]{:S(2)}) copy-start(f32[1,8,32768]{2,1,0:T(8,128)} %param.5) | copy-start | bytes 3145732
  2.6 0.9 %copy-start.1 = (f32[1,32768]{1,0:T(1,128)S(1)}, f32[1,32768]{1,0:T(1,128)}, u32[]{:S(2)}) copy-start(f32[1,32768]{1,0:T(1,128)} %param.6) | copy-start | bytes 393220
  3.5 0.9 %copy-start.2 = (s32[1,32768]{1,0:T(1,128)S(1)}, s32[1,32768]{1,0:T(1,128)}, u32[]{:S(2)}) copy-start(s32[1,32768]{1,0:T(1,128)} %param.7) | copy-start | bytes 393220

commit v2 on v1

v2 whole, which is shorter than its diff:
```python
import functools

import jax
import jax.numpy as jnp
from jax import lax
from jax.experimental import pallas as pl
from jax.experimental.pallas import tpu as pltpu
from jax.sharding import PartitionSpec as P

ROUNDS = 3
LANES = 128
GROUPS = 16

huber_edge = 1.5

MESH = pl.DeviceIdType.MESH


def ceil_to(value, unit):
    return (value + unit - 1) // unit * unit


def gather_lanes(table, index):
    return jnp.take_along_axis(table, index, axis=1, mode="promise_in_bounds")


def fit_group(columns, labels, tables):
    low = jnp.bitwise_and(labels, LANES - 1)
    high = jnp.right_shift(labels, 7)
    picked = gather_lanes(tables[0], low)
    for slab in range(1, len(tables)):
        picked = jnp.where(high == slab, gather_lanes(tables[slab], low), picked)
    return jnp.sum(columns * picked, axis=0, keepdims=True)


def entry_place(a, b, dim):
    shift = (a - b) % dim
    if shift <= dim // 2:
        return shift * dim + a
    return (dim - shift) * dim + b


def kernel(
    sizes,
    rows_hbm,
    depart_hbm,
    label_hbm,
    decay_ref,
    ridge_ref,
    coef_ref,
    corrected_ref,
    rows_ref,
    depart_ref,
    label_ref,
    acc,
    stats,
    betas,
    ridge_all,
    ridge_slab,
    decays,
    parts,
    totals,
    chained,
    load_sem,
    decay_send,
    decay_recv,
    part_send,
    part_recv,
    total_send,
    total_recv,
    beta_send,
    beta_recv,
):
    dim, channels, n_win, n_obs, slabs, half = sizes
    width = slabs * LANES
    packed = stats.shape[1]
    first = (n_obs - slabs) // 2
    steps = depart_ref.shape[0] // GROUPS
    chunk = GROUPS * LANES
    w = lax.axis_index("win")
    o = lax.axis_index("obs")

    barrier = pltpu.get_barrier_semaphore()
    for step in range(1, n_obs):
        pl.semaphore_signal(
            barrier, inc=1, device_id={"obs": lax.rem(o + step, n_obs)}, device_id_type=MESH
        )
    for step in range(1, n_win):
        pl.semaphore_signal(
            barrier, inc=1, device_id={"win": lax.rem(w + step, n_win)}, device_id_type=MESH
        )

    def loads(step):
        begin = pl.multiple_of(step * chunk, chunk)
        some = pl.ds(pl.multiple_of(step * GROUPS, GROUPS), GROUPS)
        return [
            pltpu.make_async_copy(
                rows_hbm.at[:, pl.ds(begin, chunk)],
                rows_ref.at[:, pl.ds(begin, chunk)],
                load_sem.at[0, step],
            ),
            pltpu.make_async_copy(depart_hbm.at[some], depart_ref.at[some], load_sem.at[1, step]),
            pltpu.make_async_copy(label_hbm.at[some], label_ref.at[some], load_sem.at[2, step]),
        ]

    def start_loads(step, carry):
        for load in loads(step):
            load.start()
        return carry

    lax.fori_loop(0, steps, start_loads, 0)

    def decay_copy(step, slot, target):
        return pltpu.make_async_remote_copy(
            src_ref=decays.at[slot],
            dst_ref=decays.at[slot],
            send_sem=decay_send.at[step],
            recv_sem=decay_recv.at[step],
            device_id={"win": target},
            device_id_type=MESH,
        )

    decays[w] = jnp.zeros((dim, width), jnp.float32)
    decays[w, :, 0:channels] = jnp.broadcast_to(decay_ref[...], (dim, channels))
    ridge_all[...] = jnp.ones_like(ridge_all)
    ridge_all[:, 0:channels] = ridge_ref[...].astype(jnp.float32)
    for slab in range(slabs):
        ridge_slab[slab] = ridge_all[:, slab * LANES : (slab + 1) * LANES]

    def tables_now(r):
        return [betas[r, slab] for slab in range(slabs)]

    def wide_row(ref, row):
        return jnp.broadcast_to(ref[pl.ds(row, 1), :], (dim, LANES))

    def accumulate(step, tables):
        fits, departs, labels = [], [], []
        columns_all = []
        for group in range(GROUPS):
            row = step * GROUPS + group
            begin = pl.multiple_of(row * LANES, LANES)
            columns = rows_ref[:, pl.ds(begin, LANES)]
            label = wide_row(label_ref, row)
            depart = wide_row(depart_ref, row)
            residual = depart
            if tables is not None:
                residual = depart - fit_group(columns, label, tables)
            weight = huber_edge / jnp.maximum(jnp.abs(residual), huber_edge)
            columns_all.append(columns)
            fits.append(columns * weight)
            departs.append(depart)
            labels.append(label)
        columns = jnp.concatenate(columns_all, axis=1)
        weighted = jnp.concatenate(fits, axis=1)
        depart = jnp.concatenate(departs, axis=1)
        label = jnp.concatenate(labels, axis=1)
        features = [weighted * columns]
        for shift in range(1, dim // 2 + 1):
            features.append(weighted * pltpu.roll(columns, shift, axis=0))
        features.append(weighted * depart)
        features = jnp.concatenate(features, axis=0)
        high = features.astype(jnp.bfloat16)
        low = (features - high.astype(jnp.float32)).astype(jnp.bfloat16)
        pair = jnp.concatenate([high, low], axis=0)
        upper = label >= half
        place = jnp.where(upper, label - half, label)
        place = place.astype(jnp.float32).astype(jnp.bfloat16)
        side = upper.astype(jnp.float32).astype(jnp.bfloat16)
        place = jnp.concatenate([place, place], axis=0)
        side = jnp.concatenate([side, side], axis=0)
        one, nought = jnp.bfloat16(1), jnp.bfloat16(0)
        is_upper = side > jnp.bfloat16(0.5)
        sides = [[], []]
        for part in range(0, 2 * packed, 2 * dim):
            tile = pair[part : part + 2 * dim]
            sides[0].append(jnp.where(is_upper, nought, tile))
            sides[1].append(jnp.where(is_upper, tile, nought))
        spread = jnp.concatenate(sides[0] + sides[1], axis=0)
        ids = lax.broadcasted_iota(jnp.int32, (half, LANES), 0)
        ids = ids.astype(jnp.float32).astype(jnp.bfloat16)
        hots = []
        for part in range(0, half, 2 * dim):
            id_tile = jnp.concatenate([ids[part : part + 2 * dim]] * GROUPS, axis=1)
            hots.append(jnp.where(id_tile == place, one, nought))
        hot = jnp.concatenate(hots, axis=0)
        acc[:, 0:half] += lax.dot_general(
            spread, hot, (((1,), (1,)), ((), ())), preferred_element_type=jnp.float32
        )

    def part_copy(r, slab, slot):
        return pltpu.make_async_remote_copy(
            src_ref=stats.at[slab],
            dst_ref=parts.at[r, slot],
            send_sem=part_send.at[r, slab],
            recv_sem=part_recv.at[r, slot],
            device_id={"obs": first + slab},
            device_id_type=MESH,
        )

    def total_copy(r, step, slot, target):
        return pltpu.make_async_remote_copy(
            src_ref=totals.at[r, slot],
            dst_ref=totals.at[r, slot],
            send_sem=total_send.at[r, step],
            recv_sem=total_recv.at[r, step],
            device_id={"win": target},
            device_id_type=MESH,
        )

    def beta_copy(r, step, slab, target):
        return pltpu.make_async_remote_copy(
            src_ref=betas.at[r, slab],
            dst_ref=betas.at[r, slab],
            send_sem=beta_send.at[r, step],
            recv_sem=beta_recv.at[r, slab],
            device_id={"obs": target},
            device_id_type=MESH,
        )

    def combine(r):
        zeros = jnp.zeros((packed, width - acc.shape[1]), jnp.float32)
        sides = []
        for side in range(2):
            begin = side * 2 * packed
            both = acc[begin : begin + packed] + acc[begin + packed : begin + 2 * packed]
            sides.append(jnp.concatenate([both, zeros], axis=1))
        whole = sides[0] + pltpu.roll(sides[1], half, axis=1)
        for slab in range(slabs):
            stats[slab] = whole[:, slab * LANES : (slab + 1) * LANES]
        for slab in range(slabs):

            @pl.when(o != first + slab)
            def _():
                part_copy(r, slab, o).start()

        for slab in range(slabs):

            @pl.when(o == first + slab)
            def _():
                parts[r, o] = stats[slab]
                for step in range(1, n_obs):
                    part_copy(r, 0, lax.rem(o + step, n_obs)).wait_recv()
                total = parts[r, 0]
                for source in range(1, n_obs):
                    total = total + parts[r, source]
                totals[r, w] = total
                for step in range(1, n_win):
                    total_copy(r, step, w, lax.rem(w + step, n_win)).start()
                for step in range(1, n_win):
                    total_copy(r, step, lax.rem(w + n_win - step, n_win), w).wait_recv()
                lanes = slice(slab * LANES, (slab + 1) * LANES)
                carried = totals[r, 0]
                for window in range(1, n_win):
                    decay = jnp.concatenate([decays[window, :, lanes]] * (packed // dim), axis=0)
                    further = decay * carried + totals[r, window]
                    carried = jnp.where(window <= w, further, carried)
                chained[...] = carried
                solve(r, slab)
                for step in range(1, n_obs):
                    beta_copy(r, step, slab, lax.rem(o + step, n_obs)).start()

        for slab in range(slabs):

            @pl.when(o != first + slab)
            def _():
                beta_copy(r, 1, slab, o).wait_recv()

        for slab in range(slabs):

            @pl.when(o != first + slab)
            def _():
                part_copy(r, slab, o).wait_send()

            @pl.when(o == first + slab)
            def _():
                for step in range(1, n_win):
                    total_copy(r, step, w, w).wait_send()
                for step in range(1, n_obs):
                    beta_copy(r, step, slab, o).wait_send()

    def solve(r, slab):
        def entry(place):
            return chained[place : place + 1, :]

        unit = {}
        scaled = {}
        inverse = []
        for column in range(dim):
            pivot = entry(entry_place(column, column, dim)) + ridge_slab[slab]
            for middle in range(column):
                pivot = pivot - unit[column, middle] * scaled[column, middle]
            inverse.append(1.0 / pivot)
            for row in range(column + 1, dim):
                value = entry(entry_place(row, column, dim))
                for middle in range(column):
                    value = value - unit[column, middle] * scaled[row, middle]
                scaled[row, column] = value
                unit[row, column] = value * inverse[column]
        forward = []
        moment = (dim // 2 + 1) * dim
        for row in range(dim):
            value = entry(moment + row)
            for middle in range(row):
                value = value - unit[row, middle] * forward[middle]
            forward.append(value)
        answer = [None] * dim
        for row in reversed(range(dim)):
            value = forward[row] * inverse[row]
            for middle in range(row + 1, dim):
                value = value - unit[middle, row] * answer[middle]
            answer[row] = value
            betas[r, slab, row : row + 1, :] = value

    acc[...] = jnp.zeros_like(acc)

    def opening_step(step, carry):
        for load in loads(step):
            load.wait()
        accumulate(step, None)
        return carry

    lax.fori_loop(0, steps, opening_step, 0)

    pl.semaphore_wait(barrier, n_obs + n_win - 2)
    for step in range(1, n_win):
        decay_copy(step, w, lax.rem(w + step, n_win)).start()
    for step in range(1, n_win):
        decay_copy(step, lax.rem(w + n_win - step, n_win), w).wait_recv()
    for step in range(1, n_win):
        decay_copy(step, w, w).wait_send()
    combine(0)

    def one_round(r, carry):
        acc[...] = jnp.zeros_like(acc)
        tables = tables_now(r - 1)

        def one_step(step, inner):
            accumulate(step, tables)
            return inner

        lax.fori_loop(0, steps, one_step, 0)
        combine(r)
        return carry

    lax.fori_loop(1, ROUNDS, one_round, 0)

    tables = tables_now(ROUNDS - 1)
    coef_ref[...] = jnp.concatenate(tables, axis=1)[:, 0:channels]

    def correct(step, carry):
        for group in range(GROUPS):
            row = step * GROUPS + group
            begin = pl.multiple_of(row * LANES, LANES)
            columns = rows_ref[:, pl.ds(begin, LANES)]
            fitted = fit_group(columns, wide_row(label_ref, row), tables)
            corrected_ref[pl.ds(row, 1), :] = depart_ref[pl.ds(row, 1), :] - fitted
        return carry

    lax.fori_loop(0, steps, correct, 0)


def body(n_win, n_obs, predictors, departures, channel, decay_rate, ridge_counts):
    channels = decay_rate.shape[1]
    dim = predictors.shape[1]
    total_rows = predictors.shape[2]
    slabs = ceil_to(channels, LANES) // LANES
    width = slabs * LANES
    packed = (dim // 2 + 2) * dim
    half = ceil_to((channels + 1) // 2, 16)
    acc_width = ceil_to(half, LANES)
    steps = total_rows // (GROUPS * LANES)
    assert n_obs >= slabs and total_rows % (GROUPS * LANES) == 0
    assert half <= 256 and acc_width < width and 2 * half <= width
    vmem = pl.BlockSpec(memory_space=pltpu.VMEM)
    hbm = pl.BlockSpec(memory_space=pltpu.HBM)
    dma = pltpu.SemaphoreType.DMA
    lines = total_rows // LANES
    coeffs, corrected = pl.pallas_call(
        functools.partial(kernel, (dim, channels, n_win, n_obs, slabs, half)),
        out_shape=(
            jax.ShapeDtypeStruct((dim, channels), jnp.float32),
            jax.ShapeDtypeStruct((lines, LANES), jnp.float32),
        ),
        in_specs=[hbm] * 3 + [vmem] * 2,
        out_specs=(vmem, vmem),
        scratch_shapes=[
            pltpu.VMEM((dim, total_rows), jnp.float32),
            pltpu.VMEM((lines, LANES), jnp.float32),
            pltpu.VMEM((lines, LANES), jnp.int32),
            pltpu.VMEM((4 * packed, acc_width), jnp.float32),
            pltpu.VMEM((slabs, packed, LANES), jnp.float32),
            pltpu.VMEM((ROUNDS, slabs, dim, LANES), jnp.float32),
            pltpu.VMEM((1, width), jnp.float32),
            pltpu.VMEM((slabs, 1, LANES), jnp.float32),
            pltpu.VMEM((n_win, dim, width), jnp.float32),
            pltpu.VMEM((ROUNDS, n_obs, packed, LANES), jnp.float32),
            pltpu.VMEM((ROUNDS, n_win, packed, LANES), jnp.float32),
            pltpu.VMEM((packed, LANES), jnp.float32),
            dma((3, steps)),
            dma((n_win,)),
            dma((n_win,)),
            dma((ROUNDS, slabs)),
            dma((ROUNDS, n_obs)),
            dma((ROUNDS, n_win)),
            dma((ROUNDS, n_win)),
            dma((ROUNDS, n_obs)),
            dma((ROUNDS, slabs)),
        ],
        compiler_params=pltpu.CompilerParams(
            collective_id=0, has_side_effects=True, vmem_limit_bytes=48 * 1024 * 1024
        ),
    )(
        predictors.reshape(dim, total_rows),
        departures.reshape(lines, LANES),
        channel.reshape(lines, LANES),
        decay_rate,
        ridge_counts,
    )
    return (coeffs[None], corrected.reshape(1, total_rows))


def solution(mesh):
    placed = (
        P("win", None, "obs"),
        P("win", "obs"),
        P("win", "obs"),
        P("win", None),
        P("win", None),
    )
    return jax.shard_map(
        functools.partial(body, mesh.shape["win"], mesh.shape["obs"]),
        mesh=mesh,
        in_specs=placed,
        out_specs=(P("win", None, None), P("win", "obs")),
        check_vma=False,
    )
```

time: 81.7 us -> 71.1 us (0.87)
  Pallas kernels: 75.9 us -> 65.3 us
    pallas_call x1, Pallas kernels: 75.9 us -> 65.3 us  [body(): pl.pallas_call(functools.partial(kernel, (dim, channels, n_win, n_obs, sl...]
where the time goes in v2:
time: 71.1 us; the launch traced here: 70.9 us
  Pallas kernels  65.3 us (92%)
  local copies, waits for them, and re-layouts  4.97 us (7%)
    pallas_call x1, Pallas kernels, body(): pl.pallas_call(functools.partial(kernel, (dim, channels, n_win, n_obs, sl...  65.3 us
    unnamed x12, local copies, waits for them, and re-layouts  4.97 us

profile of v2, /device:TPU:0, one launch (start us, length us, event | category | flops | bytes accessed | tf_op | source)
XLA Modules:
  0.0 70.9 jit_solution(992657302096686229)
XLA Ops:
  0.6 0.0 copy-start.3
  0.6 0.0 copy-start.4
  0.7 0.7 copy-done.3
  1.3 0.0 copy-done.4
  1.3 0.0 copy-start
  1.3 1.2 %copy-done = f32[1,8,32768]{2,1,0:T(8,128)S(1)} copy-done((f32[1,8,32768]{2,1,0:T(8,128)S(1)}, f32[1,8,32768]{2,1,0:T(8,128)}, u32[]{:S(2)}) %copy-start) | copy-done | bytes 1048600
  2.6 0.0 copy-start.1
  2.6 0.9 %copy-done.1 = f32[1,32768]{1,0:T(1,128)S(1)} copy-done((f32[1,32768]{1,0:T(1,128)S(1)}, f32[1,32768]{1,0:T(1,128)}, u32[]{:S(2)}) %copy-start.1) | copy-done | bytes 131096
  3.5 0.0 copy-start.2
  3.5 0.9 %copy-done.2 = s32[1,32768]{1,0:T(1,128)S(1)} copy-done((s32[1,32768]{1,0:T(1,128)S(1)}, s32[1,32768]{1,0:T(1,128)}, u32[]{:S(2)}) %copy-start.2) | copy-done | bytes 131096
  4.4 65.3 %shard_map.68 = (f32[8,300]{1,0:T(8,128)S(1)}, f32[256,128]{1,0:T(8,128)S(1)}) custom-call(f32[8,32768]{1,0:T(8,128)S(1)} %bitcast.5, f32[256,128]{1,0:T(8,128)S(1)} %bitcast.6, s32[256,128]{1,0:T(8,128)S(1)} %bitcast.7, f32[1,300]{1,0:T(1,128)S(1)} %copy-done.3, s32[1,300]{1,0:T(1,128)S(1)} %copy-done.4), custom_call_target="tpu_custom_call" | custom-call | tf_op jit(solution)/shard_map/pallas_call | solution.py:378
  69.6 0.6 copy.9
  70.2 0.7 copy.10
Async XLA Ops:
  0.6 0.7 copy-start.3
  0.6 0.7 copy-start.4
  1.3 1.2 %copy-start = (f32[1,8,32768]{2,1,0:T(8,128)S(1)}, f32[1,8,32768]{2,1,0:T(8,128)}, u32[]{:S(2)}) copy-start(f32[1,8,32768]{2,1,0:T(8,128)} %param.5) | copy-start | bytes 3145732
  2.6 0.9 %copy-start.1 = (f32[1,32768]{1,0:T(1,128)S(1)}, f32[1,32768]{1,0:T(1,128)}, u32[]{:S(2)}) copy-start(f32[1,32768]{1,0:T(1,128)} %param.6) | copy-start | bytes 393220
  3.5 0.9 %copy-start.2 = (s32[1,32768]{1,0:T(1,128)S(1)}, s32[1,32768]{1,0:T(1,128)}, u32[]{:S(2)}) copy-start(s32[1,32768]{1,0:T(1,128)} %param.7) | copy-start | bytes 393220

commit v3 on v2

--- a/solution.py
+++ b/solution.py
@@ -217,7 +217,7 @@
             device_id_type=MESH,
         )
 
-    def combine(r):
+    def combine(r, opening=False):
         zeros = jnp.zeros((packed, width - acc.shape[1]), jnp.float32)
         sides = []
         for side in range(2):
@@ -232,6 +232,12 @@
             @pl.when(o != first + slab)
             def _():
                 part_copy(r, slab, o).start()
+
+        if opening:
+            for step in range(1, n_win):
+                decay_copy(step, lax.rem(w + n_win - step, n_win), w).wait_recv()
+            for step in range(1, n_win):
+                decay_copy(step, w, w).wait_send()
 
         for slab in range(slabs):
 
@@ -324,11 +330,7 @@
     pl.semaphore_wait(barrier, n_obs + n_win - 2)
     for step in range(1, n_win):
         decay_copy(step, w, lax.rem(w + step, n_win)).start()
-    for step in range(1, n_win):
-        decay_copy(step, lax.rem(w + n_win - step, n_win), w).wait_recv()
-    for step in range(1, n_win):
-        decay_copy(step, w, w).wait_send()
-    combine(0)
+    combine(0, True)
 
     def one_round(r, carry):
         acc[...] = jnp.zeros_like(acc)

time: 71.1 us -> 68.7 us (0.966)
  Pallas kernels: 65.3 us -> 62.9 us
    pallas_call x1, Pallas kernels: 65.3 us -> 62.9 us  [body(): pl.pallas_call(functools.partial(kernel, (dim, channels, n_win, n_obs, sl...]
where the time goes in v3:
time: 68.7 us; the launch traced here: 68.5 us
  Pallas kernels  62.9 us (92%)
  local copies, waits for them, and re-layouts  4.97 us (7%)
    pallas_call x1, Pallas kernels, body(): pl.pallas_call(functools.partial(kernel, (dim, channels, n_win, n_obs, sl...  62.9 us
    unnamed x12, local copies, waits for them, and re-layouts  4.97 us

profile of v3, /device:TPU:0, one launch (start us, length us, event | category | flops | bytes accessed | tf_op | source)
XLA Modules:
  0.0 68.5 jit_solution(5443465054878160336)
XLA Ops:
  0.6 0.0 copy-start.3
  0.6 0.0 copy-start.4
  0.7 0.7 copy-done.3
  1.3 0.0 copy-done.4
  1.3 0.0 copy-start
  1.3 1.2 %copy-done = f32[1,8,32768]{2,1,0:T(8,128)S(1)} copy-done((f32[1,8,32768]{2,1,0:T(8,128)S(1)}, f32[1,8,32768]{2,1,0:T(8,128)}, u32[]{:S(2)}) %copy-start) | copy-done | bytes 1048600
  2.6 0.0 copy-start.1
  2.6 0.9 %copy-done.1 = f32[1,32768]{1,0:T(1,128)S(1)} copy-done((f32[1,32768]{1,0:T(1,128)S(1)}, f32[1,32768]{1,0:T(1,128)}, u32[]{:S(2)}) %copy-start.1) | copy-done | bytes 131096
  3.5 0.0 copy-start.2
  3.5 0.9 %copy-done.2 = s32[1,32768]{1,0:T(1,128)S(1)} copy-done((s32[1,32768]{1,0:T(1,128)S(1)}, s32[1,32768]{1,0:T(1,128)}, u32[]{:S(2)}) %copy-start.2) | copy-done | bytes 131096
  4.4 62.9 %shard_map.68 = (f32[8,300]{1,0:T(8,128)S(1)}, f32[256,128]{1,0:T(8,128)S(1)}) custom-call(f32[8,32768]{1,0:T(8,128)S(1)} %bitcast.5, f32[256,128]{1,0:T(8,128)S(1)} %bitcast.6, s32[256,128]{1,0:T(8,128)S(1)} %bitcast.7, f32[1,300]{1,0:T(1,128)S(1)} %copy-done.3, s32[1,300]{1,0:T(1,128)S(1)} %copy-done.4), custom_call_target="tpu_custom_call" | custom-call | tf_op jit(solution)/shard_map/pallas_call | solution.py:380
  67.2 0.6 copy.9
  67.8 0.7 copy.10
Async XLA Ops:
  0.6 0.7 copy-start.3
  0.6 0.7 %copy-start.4 = (s32[1,300]{1,0:T(1,128)S(1)}, s32[1,300]{1,0:T(1,128)}, u32[]{:S(2)}) copy-start(s32[1,300]{1,0:T(1,128)} %ridge_ref.1) | copy-start | bytes 3604
  1.3 1.2 %copy-start = (f32[1,8,32768]{2,1,0:T(8,128)S(1)}, f32[1,8,32768]{2,1,0:T(8,128)}, u32[]{:S(2)}) copy-start(f32[1,8,32768]{2,1,0:T(8,128)} %param.5) | copy-start | bytes 3145732
  2.6 0.9 %copy-start.1 = (f32[1,32768]{1,0:T(1,128)S(1)}, f32[1,32768]{1,0:T(1,128)}, u32[]{:S(2)}) copy-start(f32[1,32768]{1,0:T(1,128)} %param.6) | copy-start | bytes 393220
  3.5 0.9 %copy-start.2 = (s32[1,32768]{1,0:T(1,128)S(1)}, s32[1,32768]{1,0:T(1,128)}, u32[]{:S(2)}) copy-start(s32[1,32768]{1,0:T(1,128)} %param.7) | copy-start | bytes 393220
